TPU v7x, 32 devices: a whole 2x2x4 slice. The times are simulated.
32 devices in a mesh: row: 2 (over x), col: 16 (over z, y, core).
Axes of the slice: x: 2, y: 2, z: 4, core: 2. Of those that a mesh axis runs over, the one named last changes fastest.
Arguments:
- eigvecs: float32 [16384, 4096], P('row', 'col'), may hold values from -6 to 6
- v_panels: float32 [8, 16384, 256], P(None, 'row', 'col'), as said below
- t_panels: float32 [8, 256, 256], P(None, None, 'col'), as said below
Outputs:
- rotated: float32 [16384, 4096], P('row', 'col')
Inputs may be any that keep to these rules, and one draw needn't show every extreme that they name: `v_panels`: in panel k, vector j is zero in rows above k * 256 + j + 1, equals 1 in that row and is dense below it. t_panels[k] is upper triangular and V_k t_panels[k] V_k^T = I minus the product of the panel's 256 Householder reflections, each I - 2 v v^T / (v^T v), taken in the order of j; its diagonal lies in (0, 2].
All inputs are finite; a program needn't handle non-finite values.
Results may differ from a plain program's by a relative error of at most 0.00015.
Values sent between devices are 32-bit elements; how exact they have to be, the bound alone decides.
A program may use at most 192 MiB of HBM per device.

v0:
```python
import jax
import jax.numpy as jnp
from jax import lax
from jax.sharding import PartitionSpec as P

exact_precision = lax.Precision.HIGHEST


def matmul(left, right):
    return jnp.dot(left, right, preferred_element_type=jnp.float32, precision=exact_precision)


def project(left, right):
    return lax.dot_general(
        left,
        right,
        (((0,), (0,)), ((), ())),
        precision=exact_precision,
        preferred_element_type=jnp.float32,
    )


def local(eigvecs, v_panels, t_panels):
    panels_total = v_panels.shape[0]
    every_v, every_t = (
        lax.all_gather(v_panels, "col", axis=2, tiled=True),
        lax.all_gather(t_panels, "col", axis=2, tiled=True),
    )
    current = eigvecs
    for panel_index in reversed(range(panels_total)):
        vectors = every_v[panel_index]
        factor = every_t[panel_index]
        projected = lax.psum(project(vectors, current), "row")
        current = current - matmul(vectors, matmul(factor, projected))
    return current


def solution(mesh):
    in_specs = (P("row", "col"), P(None, "row", "col"), P(None, None, "col"))
    out_specs = P("row", "col")
    return jax.shard_map(local, mesh=mesh, in_specs=in_specs, out_specs=out_specs, check_vma=False)
```

profile of v0, /device:TPU:0, one launch (start us, length us, event | category | flops | bytes accessed | tf_op | source)
XLA Modules:
  0.0 791.7 jit_solution(15002217065631639125)
XLA Ops:
  8.1 329.7 %all-gather.3.cloned.1.call-done = f32[8,8192,256]{1,2,0:T(8,128)} async-done(((f32[8,8192,16]{1,2,0:T(8,128)}), f32[8,8192,256]{1,2,0:T(8,128)}) %all-gather.3.cloned.1.call-update) | async-done | bytes 67108880 | tf_op jit(solution)/shard_map/all_gather | solution.py:26
  337.7 11.4 %fusion.8 = f32[256,256]{1,0:T(8,128)} fusion(f32[8192,256]{1,0:T(8,128)} %param.3, f32[8,8192,256]{1,2,0:T(8,128)} %all-gather.3.cloned.1.call-done), kind=kOutput, calls=%fused_computation.24 | convolution fusion | flops 6442450944 | bytes 17039360 | tf_op jit(solution)/shard_map/dot_general | solution.py:14
  349.5 8.9 %copy.4 = f32[8192,256]{0,1:T(8,128)} copy(f32[8192,256]{1,0:T(8,128)} %param.3) | data formatting | bytes 16777216 | tf_op args[0]
  358.4 23.0 %all-gather.5.cloned.1.call-done = f32[8,256,256]{1,2,0:T(8,128)} async-done(((f32[8,256,16]{1,2,0:T(8,128)}), f32[8,256,256]{1,2,0:T(8,128)}) %all-gather.5.cloned.1.call-update) | async-done | bytes 2097168 | tf_op jit(solution)/shard_map/all_gather | solution.py:27
  381.4 24.3 %all-reduce.9.cloned.1.call-done = f32[256,256]{1,0:T(8,128)} async-done(((f32[256,256]{1,0:T(8,128)}), f32[256,256]{1,0:T(8,128)}) %all-reduce.9.cloned.1.call-update) | async-done | bytes 262160 | tf_op jit(solution)/shard_map/psum | solution.py:33
  407.4 11.9 %fusion.7 = f32[8192,256]{0,1:T(8,128)S(1)} fusion(f32[8192,256]{0,1:T(8,128)} %copy.4, f32[256,256]{1,0:T(8,128)S(1)} %fusion.30, f32[8,8192,256]{1,2,0:T(8,128)} %all-gather.3.cloned.1.call-done), kind=kOutput, calls=%fused_computation.15 | convolution fusion | flops 6444548096 | bytes 25427968 | tf_op jit(solution)/shard_map/dot_general | solution.py:10
  419.3 3.4 copy-done
  422.7 10.3 %fusion.22 = f32[256,256]{0,1:T(8,128)} fusion(f32[8192,256]{0,1:T(8,128)S(1)} %fusion.7, f32[8,8192,256]{1,2,0:T(8,128)} %all-gather.3.cloned.1.call-done), kind=kOutput, calls=%fused_computation.38 | convolution fusion | flops 6442450944 | bytes 17039360 | tf_op jit(solution)/shard_map/dot_general | solution.py:14
  433.3 23.1 %all-reduce.11.cloned.1.call-done = f32[256,256]{0,1:T(8,128)} async-done(((f32[256,256]{0,1:T(8,128)}), f32[256,256]{0,1:T(8,128)}) %all-reduce.11.cloned.1.call-update) | async-done | bytes 262160 | tf_op jit(solution)/shard_map/psum | solution.py:33
  457.8 11.9 %fusion.6 = f32[8192,256]{0,1:T(8,128)S(1)} fusion(f32[8192,256]{0,1:T(8,128)} %copy-done, f32[256,256]{1,0:T(8,128)S(1)} %fusion.29, f32[8,8192,256]{1,2,0:T(8,128)} %all-gather.3.cloned.1.call-done), kind=kOutput, calls=%fused_computation.13 | convolution fusion | flops 6444548096 | bytes 25427968 | tf_op jit(solution)/shard_map/dot_general | solution.py:10
  469.7 3.4 copy-done.1
  473.1 10.1 %fusion.21 = f32[256,256]{0,1:T(8,128)} fusion(f32[8192,256]{0,1:T(8,128)S(1)} %fusion.6, f32[8,8192,256]{1,2,0:T(8,128)} %all-gather.3.cloned.1.call-done), kind=kOutput, calls=%fused_computation.37 | convolution fusion | flops 6442450944 | bytes 17039360 | tf_op jit(solution)/shard_map/dot_general | solution.py:14
  483.9 22.8 %all-reduce.13.cloned.1.call-done = f32[256,256]{0,1:T(8,128)} async-done(((f32[256,256]{0,1:T(8,128)}), f32[256,256]{0,1:T(8,128)}) %all-reduce.13.cloned.1.call-update) | async-done | bytes 262160 | tf_op jit(solution)/shard_map/psum | solution.py:33
  508.0 11.9 %fusion.5 = f32[8192,256]{0,1:T(8,128)S(1)} fusion(f32[8192,256]{0,1:T(8,128)} %copy-done.1, f32[256,256]{1,0:T(8,128)S(1)} %fusion.28, f32[8,8192,256]{1,2,0:T(8,128)} %all-gather.3.cloned.1.call-done), kind=kOutput, calls=%fused_computation.11 | convolution fusion | flops 6444548096 | bytes 25427968 | tf_op jit(solution)/shard_map/dot_general | solution.py:10
  519.9 3.4 copy-done.2
  523.3 10.1 %fusion.20 = f32[256,256]{0,1:T(8,128)} fusion(f32[8192,256]{0,1:T(8,128)S(1)} %fusion.5, f32[8,8192,256]{1,2,0:T(8,128)} %all-gather.3.cloned.1.call-done), kind=kOutput, calls=%fused_computation.36 | convolution fusion | flops 6442450944 | bytes 17039360 | tf_op jit(solution)/shard_map/dot_general | solution.py:14
  533.7 23.2 %all-reduce.15.cloned.1.call-done = f32[256,256]{0,1:T(8,128)} async-done(((f32[256,256]{0,1:T(8,128)}), f32[256,256]{0,1:T(8,128)}) %all-reduce.15.cloned.1.call-update) | async-done | bytes 262160 | tf_op jit(solution)/shard_map/psum | solution.py:33
  558.3 11.9 %fusion.4 = f32[8192,256]{0,1:T(8,128)S(1)} fusion(f32[8192,256]{0,1:T(8,128)} %copy-done.2, f32[256,256]{1,0:T(8,128)S(1)} %fusion.27, f32[8,8192,256]{1,2,0:T(8,128)} %all-gather.3.cloned.1.call-done), kind=kOutput, calls=%fused_computation.9 | convolution fusion | flops 6444548096 | bytes 25427968 | tf_op jit(solution)/shard_map/dot_general | solution.py:10
  573.6 10.1 %fusion.19 = f32[256,256]{0,1:T(8,128)} fusion(f32[8192,256]{0,1:T(8,128)S(1)} %fusion.4, f32[8,8192,256]{1,2,0:T(8,128)} %all-gather.3.cloned.1.call-done), kind=kOutput, calls=%fused_computation.35 | convolution fusion | flops 6442450944 | bytes 17039360 | tf_op jit(solution)/shard_map/dot_general | solution.py:14
  584.0 23.2 %all-reduce.17.cloned.1.call-done = f32[256,256]{0,1:T(8,128)} async-done(((f32[256,256]{0,1:T(8,128)}), f32[256,256]{0,1:T(8,128)}) %all-reduce.17.cloned.1.call-update) | async-done | bytes 262160 | tf_op jit(solution)/shard_map/psum | solution.py:33
  608.5 11.9 %fusion.3 = f32[8192,256]{0,1:T(8,128)S(1)} fusion(f32[8192,256]{0,1:T(8,128)} %copy-done.3, f32[256,256]{1,0:T(8,128)S(1)} %fusion.26, f32[8,8192,256]{1,2,0:T(8,128)} %all-gather.3.cloned.1.call-done), kind=kOutput, calls=%fused_computation.7 | convolution fusion | flops 6444548096 | bytes 25427968 | tf_op jit(solution)/shard_map/dot_general | solution.py:10
  623.8 10.1 %fusion.18 = f32[256,256]{0,1:T(8,128)} fusion(f32[8192,256]{0,1:T(8,128)S(1)} %fusion.3, f32[8,8192,256]{1,2,0:T(8,128)} %all-gather.3.cloned.1.call-done), kind=kOutput, calls=%fused_computation.34 | convolution fusion | flops 6442450944 | bytes 17039360 | tf_op jit(solution)/shard_map/dot_general | solution.py:14
  634.3 23.2 %all-reduce.19.cloned.1.call-done = f32[256,256]{0,1:T(8,128)} async-done(((f32[256,256]{0,1:T(8,128)}), f32[256,256]{0,1:T(8,128)}) %all-reduce.19.cloned.1.call-update) | async-done | bytes 262160 | tf_op jit(solution)/shard_map/psum | solution.py:33
  658.8 11.9 %fusion.2 = f32[8192,256]{0,1:T(8,128)S(1)} fusion(f32[8192,256]{0,1:T(8,128)} %copy-done.4, f32[256,256]{1,0:T(8,128)S(1)} %fusion.25, f32[8,8192,256]{1,2,0:T(8,128)} %all-gather.3.cloned.1.call-done), kind=kOutput, calls=%fused_computation.5 | convolution fusion | flops 6444548096 | bytes 25427968 | tf_op jit(solution)/shard_map/dot_general | solution.py:10
  674.1 10.1 %fusion.17 = f32[256,256]{0,1:T(8,128)} fusion(f32[8192,256]{0,1:T(8,128)S(1)} %fusion.2, f32[8,8192,256]{1,2,0:T(8,128)} %all-gather.3.cloned.1.call-done), kind=kOutput, calls=%fused_computation.33 | convolution fusion | flops 6442450944 | bytes 17039360 | tf_op jit(solution)/shard_map/dot_general | solution.py:14
  684.7 22.9 %all-reduce.21.cloned.1.call-done = f32[256,256]{0,1:T(8,128)} async-done(((f32[256,256]{0,1:T(8,128)}), f32[256,256]{0,1:T(8,128)}) %all-reduce.21.cloned.1.call-update) | async-done | bytes 262160 | tf_op jit(solution)/shard_map/psum | solution.py:33
  709.0 11.9 %fusion.1 = f32[8192,256]{0,1:T(8,128)S(1)} fusion(f32[8192,256]{0,1:T(8,128)} %copy-done.5, f32[256,256]{1,0:T(8,128)S(1)} %fusion.24, f32[8,8192,256]{1,2,0:T(8,128)} %all-gather.3.cloned.1.call-done), kind=kOutput, calls=%fused_computation.3 | convolution fusion | flops 6444548096 | bytes 25427968 | tf_op jit(solution)/shard_map/dot_general | solution.py:10
  720.9 3.4 copy-done.6
  724.3 10.1 %fusion.16 = f32[256,256]{0,1:T(8,128)} fusion(f32[8192,256]{0,1:T(8,128)S(1)} %fusion.1, f32[8,8192,256]{1,2,0:T(8,128)} %all-gather.3.cloned.1.call-done), kind=kOutput, calls=%fused_computation.32 | convolution fusion | flops 6442450944 | bytes 17039360 | tf_op jit(solution)/shard_map/dot_general | solution.py:14
  734.5 23.5 %all-reduce.23.cloned.1.call-done = f32[256,256]{0,1:T(8,128)} async-done(((f32[256,256]{0,1:T(8,128)}), f32[256,256]{0,1:T(8,128)}) %all-reduce.23.cloned.1.call-update) | async-done | bytes 262160 | tf_op jit(solution)/shard_map/psum | solution.py:33
  759.3 16.4 %fusion = f32[8192,256]{0,1:T(8,128)} fusion(f32[8192,256]{0,1:T(8,128)} %copy-done.6, f32[256,256]{1,0:T(8,128)S(1)} %fusion.23, f32[8,8192,256]{1,2,0:T(8,128)} %all-gather.3.cloned.1.call-done), kind=kOutput, calls=%fused_computation.1 | convolution fusion | flops 6444548096 | bytes 25427968 | tf_op jit(solution)/shard_map/dot_general | solution.py:10
  775.7 9.0 %copy.5 = f32[8192,256]{1,0:T(8,128)} copy(f32[8192,256]{0,1:T(8,128)} %fusion) | data formatting | bytes 16777216 | tf_op jit(solution)/shard_map/sub | solution.py:34
  (40 shorter events, 25.3 us)
Async XLA Ops:
  6.5 331.2 %all-gather.3.cloned.1.call-start = ((), (), s32[]{:S(2)}) async-start(), calls=%async_computation | async-start | bytes 71303168 | tf_op jit(solution)/shard_map/all_gather | solution.py:26
  7.3 374.2 %all-gather.5.cloned.1.call-start = ((), (), s32[]{:S(2)}) async-start(), calls=%async_computation.2 | async-start | bytes 2228224 | tf_op jit(solution)/shard_map/all_gather | solution.py:27
  8.0 397.7 %all-reduce.9.cloned.1.call-start = ((), (), s32[]{:S(2)}) async-start(), calls=%async_computation.1 | async-start | bytes 524288 | tf_op jit(solution)/shard_map/psum | solution.py:33
  349.1 107.3 %all-reduce.11.cloned.1.call-start = ((), (), s32[]{:S(2)}) async-start(), calls=%async_computation.3 | async-start | bytes 524288 | tf_op jit(solution)/shard_map/psum | solution.py:33
  419.3 3.4 copy-start
  422.7 33.8 %copy-start.7 = (f32[8,256,256]{1,2,0:T(8,128)S(1)}, f32[8,256,256]{1,2,0:T(8,128)}, u32[]{:S(2)}) copy-start(f32[8,256,256]{1,2,0:T(8,128)} %all-gather.5.cloned.1.call-done) | copy-start | bytes 6291460
  433.0 73.7 %all-reduce.13.cloned.1.call-start = ((), (), s32[]{:S(2)}) async-start(), calls=%async_computation.4 | async-start | bytes 524288 | tf_op jit(solution)/shard_map/psum | solution.py:33
  469.7 3.4 copy-start.1
  483.2 73.7 %all-reduce.15.cloned.1.call-start = ((), (), s32[]{:S(2)}) async-start(), calls=%async_computation.5 | async-start | bytes 524288 | tf_op jit(solution)/shard_map/psum | solution.py:33
  519.9 3.4 copy-start.2
  533.5 73.7 %all-reduce.17.cloned.1.call-start = ((), (), s32[]{:S(2)}) async-start(), calls=%async_computation.6 | async-start | bytes 524288 | tf_op jit(solution)/shard_map/psum | solution.py:33
  570.2 3.4 copy-start.3
  583.7 73.7 %all-reduce.19.cloned.1.call-start = ((), (), s32[]{:S(2)}) async-start(), calls=%async_computation.7 | async-start | bytes 524288 | tf_op jit(solution)/shard_map/psum | solution.py:33
  620.4 3.4 copy-start.4
  634.0 73.7 %all-reduce.21.cloned.1.call-start = ((), (), s32[]{:S(2)}) async-start(), calls=%async_computation.8 | async-start | bytes 524288 | tf_op jit(solution)/shard_map/psum | solution.py:33
  670.7 3.4 copy-start.5
  684.2 73.7 %all-reduce.23.cloned.1.call-start = ((), (), s32[]{:S(2)}) async-start(), calls=%async_computation.9 | async-start | bytes 524288 | tf_op jit(solution)/shard_map/psum | solution.py:33
  720.9 3.4 copy-start.6
Sparse Core Ops, SparseCore 0:
  8.9 328.7 all-gather.2
  339.9 41.4 all-gather.4
  383.7 22.0 all-reduce.8
  433.1 23.2 all-reduce.10
  483.3 23.2 all-reduce.12
  533.6 23.2 all-reduce.14
  583.8 23.2 all-reduce.16
  634.1 23.2 all-reduce.18
  684.3 23.2 all-reduce.20
  734.6 23.2 all-reduce.22
where the time goes:
time: 796 us; the launch traced here: 792 us
  waiting for transfers between devices  540 us (68%)
  matrix products  193 us (24%)
  local copies, waits for them, and re-layouts  41.6 us (5%)
  between operations  13.9 us (2%)
    all_gather x1, waiting for transfers between devices, local(): lax.all_gather(v_panels, 'col', axis=2, tiled=True)  330 us
    psum x8, waiting for transfers between devices, local(): projected = lax.psum(project(vectors, current), 'row')  186 us
    dot_general x16, matrix products, matmul(): jnp.dot(left, right, preferred_element_type=jnp.float32, precision=exact_...  111 us
    dot_general x8, matrix products, project(): lax.dot_general(left, right, (((0,), (0,)), ((), ())), precision=exact_pr...  82.4 us
    unnamed x17, local copies, waits for them, and re-layouts  32.7 us
    all_gather x1, waiting for transfers between devices, local(): lax.all_gather(t_panels, 'col', axis=2, tiled=True)  23 us
  transfers between devices with their start and end apart: 10, of which 10 were waited for; matrix products, arithmetic and copies ran while one was open for 3% of the time, Pallas kernels for 0%

commit v1 on v0

v1 whole, which is shorter than its diff:
```python
import functools

import jax
import jax.numpy as jnp
from jax import lax
from jax.experimental import pallas as pl
from jax.experimental.pallas import tpu as pltpu
from jax.sharding import PartitionSpec as P

SLOTS = 4
MESH = pl.DeviceIdType.MESH


def halves(x):
    high = x.astype(jnp.bfloat16)
    return high, (x - high.astype(jnp.float32)).astype(jnp.bfloat16)


def dot3(left, right, left_axis, right_axis):
    def one(a, b):
        return lax.dot_general(
            a, b, (((left_axis,), (right_axis,)), ((), ())), preferred_element_type=jnp.float32
        )

    (lh, ll), (rh, rl) = left, right
    return one(lh, rh) + (one(ll, rh) + one(lh, rl))


def kernel(shape, z_hbm, p_ref, out_ref, g_ref, zbuf, vbuf, acc, psend, precv, *sems):
    panels, width, rows, groups, A, B = shape
    recv, su, sd, sy, sc, lsem, zsem, psnd, prcv = sems
    per = p_ref.shape[1]
    length = p_ref.shape[2]
    tiles = length // 128
    cut = (tiles - tiles // 6) * 128
    lanes = (pl.ds(0, cut), pl.ds(cut, length - cut))
    tile = min(rows, 1024)
    me = lax.axis_index("col")
    my_row = lax.axis_index("row")
    c = lax.rem(me, 2)
    b = lax.rem(me // 2, B)
    a = me // (2 * B)

    def index(aa, bb, cc):
        return (aa * B + bb) * 2 + cc

    def walk(i, s, go):
        k = panels - 1 - i
        sl = lax.rem(i, SLOTS)

        def place(owner, q):
            return g_ref.at[k, pl.ds(pl.multiple_of(owner * per, per), per), lanes[q]]

        def move(owner, q, own, target, sem):
            copy = pltpu.make_async_remote_copy(
                src_ref=p_ref.at[k, :, lanes[q]] if own else place(owner, q),
                dst_ref=place(owner, q),
                send_sem=sem,
                recv_sem=recv.at[sl, q, owner],
                device_id={"col": target},
                device_id_type=MESH,
            )
            if go:
                copy.start()
            else:
                copy.wait_send()

        def arrive(owner, q):
            if go:
                pltpu.make_async_remote_copy(
                    src_ref=place(owner, q),
                    dst_ref=place(owner, q),
                    send_sem=sc.at[sl, q, 0],
                    recv_sem=recv.at[sl, q, owner],
                    device_id={"col": index(a, b, 1 - c)},
                    device_id_type=MESH,
                ).wait_recv()

        def along(sg, owner, q, own, cid):
            if sg >= 0:

                @pl.when(a < A - 1)
                def _():
                    move(owner, q, own, index(a + 1, b, c), su.at[sl, q, cid])

            if sg <= 0:

                @pl.when(a > 0)
                def _():
                    move(owner, q, own, index(a - 1, b, c), sd.at[sl, q, cid])

        def across(owner, q, own, slot):
            for j in range(1, B):
                move(owner, q, own, index(a, lax.rem(b + j, B), c), sy.at[sl, slot, j - 1])

        def over(owner, q, own, cid):
            move(owner, q, own, index(a, b, 1 - c), sc.at[sl, q, cid])

        def signs(d):
            return (1, -1) if d else (0,)

        if s < A:
            for sg in signs(s):
                at = a - sg * s

                @pl.when((at >= 0) & (at < A))
                def _(sg=sg, at=at):
                    owner, cid, own = index(at, b, c), at * B + b, s == 0
                    if not own:
                        arrive(owner, 0)
                    along(sg, owner, 0, own, cid)
                    across(owner, 0, own, at)
                    over(owner, 0, own, cid)

        if s == 0:
            across(me, 1, True, A)
            along(0, me, 1, True, a * B + b)
            over(me, 1, True, a * B + b)
        else:
            for sg in signs(s - 1):
                at = a - sg * (s - 1)

                @pl.when((at >= 0) & (at < A))
                def _(sg=sg, at=at):
                    for j in range(B):
                        if s == 1 and j == 0:
                            continue
                        bb = lax.rem(b + j, B)
                        owner, cid = index(at, bb, c), at * B + bb
                        arrive(owner, 1)
                        along(sg, owner, 1, False, cid)
                        over(owner, 1, False, cid)
                    for j in range(1, B):
                        bb = lax.rem(b + j, B)
                        owner, cid = index(at, bb, c), at * B + bb
                        arrive(owner, 0)
                        over(owner, 0, False, cid)

    def settle(i):
        k = panels - 1 - i
        sl = lax.rem(i, SLOTS)
        for at in range(A):
            for bb in range(B):
                owner = index(at, bb, 1 - c)
                for q in range(2):
                    spot = g_ref.at[k, pl.ds(pl.multiple_of(owner * per, per), per), lanes[q]]
                    pltpu.make_async_remote_copy(
                        src_ref=spot,
                        dst_ref=spot,
                        send_sem=sc.at[sl, q, 0],
                        recv_sem=recv.at[sl, q, owner],
                        device_id={"col": index(a, b, 1 - c)},
                        device_id_type=MESH,
                    ).wait_recv()

    def load(i):
        k = panels - 1 - i
        sl = lax.rem(i, 2)
        for owner in range(A * B * 2):
            spot = pl.ds(owner * per, per)

            @pl.when(me == owner)
            def _():
                pltpu.make_async_copy(p_ref.at[k], vbuf.at[sl, spot], lsem.at[sl]).start()

            @pl.when(me != owner)
            def _():
                pltpu.make_async_copy(g_ref.at[k, spot], vbuf.at[sl, spot], lsem.at[sl]).start()

    def partial(sl, j):
        return pltpu.make_async_remote_copy(
            src_ref=psend.at[sl],
            dst_ref=precv.at[sl, j - 1],
            send_sem=psnd.at[sl, j - 1],
            recv_sem=prcv.at[sl, j - 1],
            device_id={"row": lax.rem(my_row + j, groups)},
            device_id_type=MESH,
        )

    def project(i):
        k = panels - 1 - i
        sl = lax.rem(i, 2)
        pltpu.make_async_copy(g_ref.at[k], vbuf.at[sl], lsem.at[sl]).wait()
        acc[...] = jnp.zeros_like(acc)

        def body(n, _):
            at = pl.multiple_of(n * tile, tile)
            left = halves(vbuf[sl, :, pl.ds(at, tile)])
            right = halves(zbuf[pl.ds(at, tile), :])
            acc[...] += dot3(left, right, 1, 0)
            return 0

        lax.fori_loop(0, rows // tile, body, 0)
        psend[sl] = acc[...]
        for j in range(1, groups):
            partial(sl, j).start()

    def update(i):
        sl = lax.rem(i, 2)
        total = acc[...]
        for j in range(1, groups):
            partial(sl, j).wait()
            total = total + precv[sl, j - 1]
        factor = halves(vbuf[sl, :, pl.ds(rows, width)])
        scaled = halves(dot3(factor, halves(total), 0, 0))

        def body(n, _):
            at = pl.multiple_of(n * tile, tile)
            left = halves(vbuf[sl, :, pl.ds(at, tile)])
            zbuf[pl.ds(at, tile), :] = zbuf[pl.ds(at, tile), :] - dot3(left, scaled, 0, 0)
            return 0

        lax.fori_loop(0, rows // tile, body, 0)

    fetch = pltpu.make_async_copy(z_hbm, zbuf, zsem)
    fetch.start()
    walk(0, 0, True)
    fetch.wait()

    def iteration(i, _):
        @pl.when(i > 0)
        def _():
            walk(i - 1, A, True)
            settle(i - 1)
            load(i - 1)

        @pl.when(i < panels)
        def _():
            walk(i, 1, True)

        @pl.when(i > 0)
        def _():
            project(i - 1)

        @pl.when(i + 1 < panels)
        def _():
            walk(i + 1, 0, True)

        @pl.when(i < panels)
        def _():
            for s in range(2, A - 1):
                walk(i, s, True)

        @pl.when(i > 0)
        def _():
            update(i - 1)

        @pl.when(i < panels)
        def _():
            walk(i, A - 1, True)

        @pl.when(i > 0)
        def _():
            for s in range(A + 1):
                walk(i - 1, s, False)

        return 0

    lax.fori_loop(0, panels + 1, iteration, 0)
    store = pltpu.make_async_copy(zbuf, out_ref, zsem)
    store.start()
    store.wait()


def local(eigvecs, v_panels, t_panels):
    panels, rows, per = v_panels.shape
    width = t_panels.shape[1]
    groups = lax.axis_size("row")
    members = lax.axis_size("col")
    chips = members // 2
    B = max(n for n in range(1, chips + 1) if chips % n == 0 and n * n <= chips)
    A = chips // B
    columns = eigvecs.shape[1]
    packed = jnp.concatenate(
        [jnp.transpose(v_panels, (0, 2, 1)), jnp.transpose(t_panels, (0, 2, 1))], axis=2
    )
    length = rows + width
    dma = pltpu.SemaphoreType.DMA
    anywhere = pl.BlockSpec(memory_space=pl.ANY)
    others = max(groups - 1, 1)
    out, _ = pl.pallas_call(
        functools.partial(kernel, (panels, width, rows, groups, A, B)),
        out_shape=(
            jax.ShapeDtypeStruct((rows, columns), jnp.float32),
            jax.ShapeDtypeStruct((panels, width, length), jnp.float32),
        ),
        in_specs=[anywhere] * 2,
        out_specs=(anywhere, anywhere),
        scratch_shapes=[
            pltpu.VMEM((rows, columns), jnp.float32),
            pltpu.VMEM((2, width, length), jnp.float32),
            pltpu.VMEM((width, columns), jnp.float32),
            pltpu.VMEM((2, width, columns), jnp.float32),
            pltpu.VMEM((2, others, width, columns), jnp.float32),
            dma((SLOTS, 2, members)),
            dma((SLOTS, 2, chips)),
            dma((SLOTS, 2, chips)),
            dma((SLOTS, A + 1, max(B - 1, 1))),
            dma((SLOTS, 2, chips)),
            dma((2,)),
            dma,
            dma((2, others)),
            dma((2, others)),
        ],
        compiler_params=pltpu.CompilerParams(has_side_effects=True, vmem_limit_bytes=60 * 2**20),
    )(eigvecs, packed)
    return out


def solution(mesh):
    in_specs = (P("row", "col"), P(None, "row", "col"), P(None, None, "col"))
    out_specs = P("row", "col")
    return jax.shard_map(local, mesh=mesh, in_specs=in_specs, out_specs=out_specs, check_vma=False)
```

time: 796 us -> 413 us (0.52)
  waiting for transfers between devices: 540 us -> 0 us
  Pallas kernels: 0 us -> 400 us
  matrix products: 193 us -> 0 us
  local copies, waits for them, and re-layouts: 41.6 us -> 7.32 us
  between operations: 13.9 us -> 0.01 us
    pallas_call x0 -> x1, Pallas kernels: none -> 400 us  [local(): pl.pallas_call(functools.partial(kernel, (panels, width, rows, groups, A,...]
    all_gather x2 -> x0, waiting for transfers between devices: 353 us -> none  [the longest x1 330 us: local(): lax.all_gather(v_panels, 'col', axis=2, tiled=True)]
    dot_general x24 -> x0, matrix products: 193 us -> none  [the longest x16 111 us: matmul(): jnp.dot(left, right, preferred_element_type=jnp.float32, precision=exact_...]
    psum x8 -> x0, waiting for transfers between devices: 186 us -> none  [local(): projected = lax.psum(project(vectors, current), 'row')]
    unnamed x17 -> x1, local copies, waits for them, and re-layouts: 32.7 us -> 7.32 us
    sub x1 -> x0, local copies, waits for them, and re-layouts: 8.99 us -> none  [local(): current = current - matmul(vectors, matmul(factor, projected))]
  transfers between devices with their start and end apart: 10 -> 0, of which waited for: 10 -> 0; matrix products, arithmetic and copies ran while one was open for 3% -> 0% of each run, Pallas kernels for 0% -> 0%
where the time goes in v1:
time: 413 us; the launch traced here: 412 us
  Pallas kernels  400 us (97%)
  local copies, waits for them, and re-layouts  7.32 us (2%)
  other arithmetic  4.69 us (1%)
    pallas_call x1, Pallas kernels, local(): pl.pallas_call(functools.partial(kernel, (panels, width, rows, groups, A,...  400 us

profile of v1, /device:TPU:0, one launch (start us, length us, event | category | flops | bytes accessed | tf_op | source)
XLA Modules:
  0.0 412.5 jit_solution(13306777600266051449)
XLA Ops:
  0.0 4.7 %pad_maximum_fusion.p_ref = f32[8,16,8448]{2,1,0:T(8,128)} fusion(f32[8,16,256]{2,1,0:T(8,128)} %bitcast.3, f32[8,16,8192]{2,1,0:T(8,128)} %bitcast.2), kind=kLoop, calls=%fused_computation | loop fusion | flops 1081344 | bytes 8650752 | tf_op jit(solution)/shard_map/concatenate | solution.py:274
  4.7 400.5 %shard_map.37 = (f32[8192,256]{1,0:T(8,128)}, f32[8,256,8448]{2,1,0:T(8,128)}) custom-call(f32[8192,256]{1,0:T(8,128)} %z_hbm.1, f32[8,16,8448]{2,1,0:T(8,128)} %pad_maximum_fusion.p_ref), custom_call_target="tpu_custom_call" | custom-call | tf_op jit(solution)/shard_map/pallas_call | solution.py:281
  405.2 7.3 %copy.5 = f32[8192,256]{1,0:T(8,128)} copy(f32[8192,256]{1,0:T(8,128)} %get-tuple-element.6) | data formatting | bytes 16777216

commit v2 on v1

--- a/solution.py
+++ b/solution.py
@@ -32,7 +32,7 @@
     per = p_ref.shape[1]
     length = p_ref.shape[2]
     tiles = length // 128
-    cut = (tiles - tiles // 6) * 128
+    cut = (tiles - tiles // 4) * 128
     lanes = (pl.ds(0, cut), pl.ds(cut, length - cut))
     tile = min(rows, 1024)
     me = lax.axis_index("col")
@@ -195,6 +195,10 @@
         for j in range(1, groups):
             partial(sl, j).start()
 
+    def store(n):
+        spot = pl.ds(pl.multiple_of(n * tile, tile), tile)
+        return pltpu.make_async_copy(zbuf.at[spot], out_ref.at[spot], zsem)
+
     def update(i):
         sl = lax.rem(i, 2)
         total = acc[...]
@@ -208,6 +212,11 @@
             at = pl.multiple_of(n * tile, tile)
             left = halves(vbuf[sl, :, pl.ds(at, tile)])
             zbuf[pl.ds(at, tile), :] = zbuf[pl.ds(at, tile), :] - dot3(left, scaled, 0, 0)
+
+            @pl.when((i == panels - 1) & (n > 0))
+            def _():
+                store(n - 1).start()
+
             return 0
 
         lax.fori_loop(0, rows // tile, body, 0)
@@ -218,36 +227,39 @@
     fetch.wait()
 
     def iteration(i, _):
+        @pl.when(i < panels)
+        def _():
+            walk(i, 1, True)
+
         @pl.when(i > 0)
         def _():
             walk(i - 1, A, True)
+
+        @pl.when(i + 1 < panels)
+        def _():
+            walk(i + 1, 0, True)
+
+        @pl.when(i > 0)
+        def _():
             settle(i - 1)
             load(i - 1)
 
         @pl.when(i < panels)
         def _():
-            walk(i, 1, True)
-
-        @pl.when(i > 0)
-        def _():
-            project(i - 1)
-
-        @pl.when(i + 1 < panels)
-        def _():
-            walk(i + 1, 0, True)
-
-        @pl.when(i < panels)
-        def _():
             for s in range(2, A - 1):
                 walk(i, s, True)
 
         @pl.when(i > 0)
         def _():
+            project(i - 1)
+
+        @pl.when(i < panels)
+        def _():
+            walk(i, A - 1, True)
+
+        @pl.when(i > 0)
+        def _():
             update(i - 1)
-
-        @pl.when(i < panels)
-        def _():
-            walk(i, A - 1, True)
 
         @pl.when(i > 0)
         def _():
@@ -257,9 +269,8 @@
         return 0
 
     lax.fori_loop(0, panels + 1, iteration, 0)
-    store = pltpu.make_async_copy(zbuf, out_ref, zsem)
-    store.start()
-    store.wait()
+    store(rows // tile - 1).start()
+    pltpu.make_async_copy(zbuf, out_ref, zsem).wait()
 
 
 def local(eigvecs, v_panels, t_panels):

time: 413 us -> 396 us (0.959)
  Pallas kernels: 400 us -> 383 us
    pallas_call x1, Pallas kernels: 400 us -> 383 us  [local(): pl.pallas_call(functools.partial(kernel, (panels, width, rows, groups, A,...]
where the time goes in v2:
time: 396 us; the launch traced here: 395 us
  Pallas kernels  383 us (97%)
  local copies, waits for them, and re-layouts  7.32 us (2%)
  other arithmetic  4.69 us (1%)
    pallas_call x1, Pallas kernels, local(): pl.pallas_call(functools.partial(kernel, (panels, width, rows, groups, A,...  383 us

profile of v2, /device:TPU:0, one launch (start us, length us, event | category | flops | bytes accessed | tf_op | source)
XLA Modules:
  0.0 394.9 jit_solution(7626380581532824363)
XLA Ops:
  0.0 4.7 %pad_maximum_fusion.p_ref = f32[8,16,8448]{2,1,0:T(8,128)} fusion(f32[8,16,256]{2,1,0:T(8,128)} %bitcast.3, f32[8,16,8192]{2,1,0:T(8,128)} %bitcast.2), kind=kLoop, calls=%fused_computation | loop fusion | flops 1081344 | bytes 8650752 | tf_op jit(solution)/shard_map/concatenate | solution.py:285
  4.7 382.9 %shard_map.37 = (f32[8192,256]{1,0:T(8,128)}, f32[8,256,8448]{2,1,0:T(8,128)}) custom-call(f32[8192,256]{1,0:T(8,128)} %z_hbm.1, f32[8,16,8448]{2,1,0:T(8,128)} %pad_maximum_fusion.p_ref), custom_call_target="tpu_custom_call" | custom-call | tf_op jit(solution)/shard_map/pallas_call | solution.py:292
  387.6 7.3 %copy.5 = f32[8192,256]{1,0:T(8,128)} copy(f32[8192,256]{1,0:T(8,128)} %get-tuple-element.6) | data formatting | bytes 16777216
